TPU v7x, 32 devices: a whole 2x2x4 slice. The times are simulated.
32 devices in a mesh: row: 8 (over y, x, core), col: 4 (over z).
Axes of the slice: x: 2, y: 2, z: 4, core: 2. Of those that a mesh axis runs over, the one named last changes fastest.
Arguments:
- tokens: bfloat16 [1024, 8192], P('row', 'col'), may hold values from -200 to 200
- norm_gain: float32 [8192], P('col'), may hold values from 0.1 to 1.9
- gate_weight: bfloat16 [8192, 28672], P('col', 'row'), may hold values from -0.0625 to 0.0625
- up_weight: bfloat16 [8192, 28672], P('col', 'row'), may hold values from -0.0625 to 0.0625
- down_weight: bfloat16 [28672, 8192], P('row', 'col'), may hold values from -0.03125 to 0.03125
Outputs:
- mixed: bfloat16 [1024, 8192], P('row', 'col')
All inputs are finite; a program needn't handle non-finite values.
Results may differ from a plain program's by a relative error of at most 0.028.
Values may be sent and summed in bfloat16 or wider, within the bound.
A program may use at most 128 MiB of HBM per device.

v0:
```python
import functools

import jax
import jax.numpy as jnp
from jax import lax
from jax.experimental import pallas as pl
from jax.experimental.pallas import tpu as pltpu
from jax.sharding import PartitionSpec as P

MESH = pl.DeviceIdType.MESH
LAG_SUM = 2
LAG_HID = 1
STAGES = 4
KEEP = 2
PIECES = 4


def exclusive_or(a, b, bits):
    total = a + b
    for bit in range(bits):
        size = 1 << bit
        total = total - 2 * size * (((a // size) % 2) * ((b // size) % 2))
    return total


def kernel(
    plan, tok, gain, gate_w, up_w, down_w, out,
    xall, wgu, wd, gu_in, gu_out, ybuf, hid, acc, own, rs_in, rs_out,
    sq_out, sq_in, tot_out, tot_in, scale,
    own_sem, wg_sem, wu_sem, wd_sem, ag_send, ag_recv, rs_send, rs_recv,
    sq_send, sq_recv, tot_send, tot_recv, gs_send, gs_recv, hs_send, hs_recv,
):
    rows, cols, part, depth, width, chunks = plan
    hops = cols - 1
    units = rows * chunks
    half = chunks * width
    lag = hops * (LAG_SUM + LAG_HID)
    slots = gu_in.shape[1]
    places = hid.shape[1]
    banks = acc.shape[0]
    bits = rows.bit_length() - 1
    r, p = lax.axis_index("row"), lax.axis_index("col")
    spot = (p, hops - p)
    after = (p + 1, p - 1)
    before = (p - 1, p + 1)
    near = jnp.minimum(spot[0], spot[1])
    far = hops - near

    def mask(i):
        if isinstance(i, int):
            return 0 if i == 0 else (1 if i == rows - 1 else i + 1)
        return jnp.where(i == 0, 0, jnp.where(i == rows - 1, 1, i + 1))

    def partner(i):
        return exclusive_or(r, mask(i), bits)

    def weight_copies(s, j):
        at = s * half + j * width
        c = s * chunks + j
        return (
            pltpu.make_async_copy(gate_w.at[:, pl.ds(at, width)], wgu.at[c, :, pl.ds(0, width)], wg_sem.at[c]),
            pltpu.make_async_copy(up_w.at[:, pl.ds(at, width)], wgu.at[c, :, pl.ds(width, width)], wu_sem.at[c]),
        )

    def down_copy(s, j):
        c = s * chunks + j
        return pltpu.make_async_copy(down_w.at[pl.ds(s * half + j * width, width)], wd.at[c], wd_sem.at[c])

    own_copy = pltpu.make_async_copy(tok, xall.at[0], own_sem)
    own_copy.start()
    for s in (0, 1):
        for one in weight_copies(s, 0):
            one.start()

    barrier = pltpu.get_barrier_semaphore()
    for i in range(1, rows):
        pl.semaphore_signal(barrier, inc=1, device_id=(partner(i), p), device_id_type=MESH)
    for d in range(1, cols):
        pl.semaphore_signal(barrier, inc=1, device_id=(r, (p + d) % cols), device_id_type=MESH)
    pl.semaphore_wait(barrier, rows + cols - 2)

    def spread(i):
        return pltpu.make_async_remote_copy(
            src_ref=tok, dst_ref=xall.at[i], send_sem=ag_send.at[i], recv_sem=ag_recv.at[i],
            device_id=(partner(i), p), device_id_type=MESH)

    for i in range(1, rows):
        spread(i).start()
    for j in range(1, chunks):
        for s in (0, 1):
            for one in weight_copies(s, j):
                one.start()
    for j in range(chunks):
        for s in (0, 1):
            down_copy(s, j).start()

    def square_copy(d):
        return pltpu.make_async_remote_copy(
            src_ref=sq_out, dst_ref=sq_in.at[d], send_sem=sq_send.at[d], recv_sem=sq_recv.at[d],
            device_id=(r, (p + d) % cols), device_id_type=MESH)

    def total_copy(i):
        return pltpu.make_async_remote_copy(
            src_ref=tot_out, dst_ref=tot_in.at[i], send_sem=tot_send.at[i], recv_sem=tot_recv.at[i],
            device_id=(partner(i), p), device_id_type=MESH)

    own_copy.wait()
    squares = jnp.zeros((part, 128), jnp.float32)
    for c in range(depth // 128):
        at = pl.ds(c * 128, 128)
        value = xall[0, :, at].astype(jnp.float32)
        squares = squares + value * value
        xall[0, :, at] = (value * gain[:, at]).astype(jnp.bfloat16)
    sq_out[...] = jnp.broadcast_to(jnp.sum(squares.T, axis=0, keepdims=True), (8, part))
    for d in range(1, cols):
        square_copy(d).start()

    def put_scale(i, total):
        tall = jnp.broadcast_to(total[0:1, :], (128, part)).T
        scale[i] = lax.rsqrt(tall / (depth * cols) + 1e-05)

    def total_squares():
        total = sq_out[...]
        for d in range(1, cols):
            square_copy(d).wait_recv()
            total = total + sq_in[d]
        tot_out[...] = total
        put_scale(0, total)
        for i in range(1, rows):
            total_copy(i).start()

    def sum_copy(s, n):
        stage, slot = lax.rem(n, STAGES), lax.rem(n, slots)
        return pltpu.make_async_remote_copy(
            src_ref=gu_out.at[s, stage], dst_ref=gu_in.at[s, slot],
            send_sem=gs_send.at[s, stage], recv_sem=gs_recv.at[s, slot],
            device_id=(r, after[s]), device_id_type=MESH)

    def hidden_copy(s, m):
        place = lax.rem(m, places)
        return pltpu.make_async_remote_copy(
            src_ref=hid.at[s, place], dst_ref=hid.at[s, place],
            send_sem=hs_send.at[s, place], recv_sem=hs_recv.at[s, place],
            device_id=(r, before[s]), device_id_type=MESH)

    def result_copy(i):
        return pltpu.make_async_remote_copy(
            src_ref=rs_out, dst_ref=rs_in.at[i], send_sem=rs_send, recv_sem=rs_recv.at[i],
            device_id=(partner(i), p), device_id_type=MESH)

    def sums(s, t):
        q = spot[s]
        n = t - LAG_SUM * q
        valid = (n >= 0) & (n < units)

        @pl.when(valid)
        def _():
            i = n // chunks
            j = n - i * chunks

            @pl.when(i == 0)
            def _():
                for one in weight_copies(s, j):
                    one.wait()

            ybuf[...] = jnp.dot(xall[i], wgu[s * chunks + j], preferred_element_type=jnp.float32)

            @pl.when(q > 0)
            def _():
                sum_copy(s, n).wait_recv()
                ybuf[...] += gu_in[s, lax.rem(n, slots)].astype(jnp.float32)

        @pl.when((q < hops) & (n >= STAGES) & (n < units + STAGES))
        def _():
            sum_copy(s, n - STAGES).wait_send()

        @pl.when(valid & (q < hops))
        def _():
            gu_out[s, lax.rem(n, STAGES)] = ybuf[...].astype(jnp.bfloat16)
            sum_copy(s, n).start()

        @pl.when(valid & (q == hops))
        def _():
            factor = scale[n // chunks]
            for c in range(width // 128):
                g = ybuf[:, pl.ds(c * 128, 128)] * factor
                u = ybuf[:, pl.ds(width + c * 128, 128)] * factor
                hid[s, lax.rem(n, places), :, pl.ds(c * 128, 128)] = (jax.nn.silu(g) * u).astype(jnp.bfloat16)
            hidden_copy(s, n).start()

    def hiddens(s, t):
        q = spot[s]
        m = t - lag + LAG_HID * q
        valid = (m >= 0) & (m < units)
        place = lax.rem(jnp.maximum(m, 0), places)

        @pl.when(valid & (q < hops))
        def _():
            hidden_copy(s, m).wait_recv()

        @pl.when(valid & (q < hops) & (q > 0))
        def _():
            hidden_copy(s, m).start()

        @pl.when(valid)
        def _():
            i = m // chunks
            j = m - i * chunks
            bank = lax.rem(i, banks)

            @pl.when(i == 0)
            def _():
                down_copy(s, j).wait()

            leads = (q == far) if s == 0 else ((q == far) & (spot[0] != far))
            fresh = leads & (j == 0)
            wide = depth // PIECES
            for c in range(PIECES):
                at = pl.ds(c * wide, wide)
                value = jnp.dot(hid[s, place], wd[s * chunks + j, :, at], preferred_element_type=jnp.float32)

                @pl.when(fresh)
                def _():
                    acc[bank, :, at] = value

                @pl.when(jnp.logical_not(fresh))
                def _():
                    acc[bank, :, at] += value

        @pl.when((q > 0) & (m >= KEEP) & (m < units + KEEP))
        def _():
            hidden_copy(s, m - KEEP).wait_send()

    def step(t, carry):
        first = t - LAG_SUM * near

        @pl.when((first >= chunks) & (first < units) & (first % chunks == 0))
        def _():
            i = first // chunks
            spread(i).wait_recv()
            total_copy(i).wait_recv()
            for c in range(depth // 128):
                at = pl.ds(c * 128, 128)
                xall[i, :, at] = (xall[i, :, at].astype(jnp.float32) * gain[:, at]).astype(jnp.bfloat16)
            put_scale(i, tot_in[i])

        sums(0, t)
        sums(1, t)

        @pl.when(first == 1)
        def _():
            total_squares()

        hiddens(0, t)
        hiddens(1, t)

        last = t - lag + LAG_HID * near

        @pl.when((last >= 0) & (last < units) & (last % chunks == chunks - 1))
        def _():
            i = last // chunks
            bank = lax.rem(i, banks)

            @pl.when(i == 0)
            def _():
                own[...] = acc[bank]

            @pl.when(i >= 2)
            def _():
                result_copy(i - 1).wait_send()

            @pl.when(i > 0)
            def _():
                rs_out[...] = acc[bank].astype(jnp.bfloat16)
                result_copy(i).start()

            @pl.when(i >= 2)
            def _():
                result_copy(i - 1).wait_recv()
                own[...] += rs_in[i - 1].astype(jnp.float32)

        return carry

    lax.fori_loop(0, units + lag + KEEP, step, 0)

    if rows > 1:
        result_copy(rows - 1).wait_send()
        result_copy(rows - 1).wait_recv()
        out[...] = (own[...] + rs_in[rows - 1].astype(jnp.float32)).astype(jnp.bfloat16)
    else:
        out[...] = own[...].astype(jnp.bfloat16)
    for i in range(1, rows):
        spread(i).wait_send()
        total_copy(i).wait_send()
    for d in range(1, cols):
        square_copy(d).wait_send()


def make_body(rows, cols):
    hops = cols - 1
    assert rows & (rows - 1) == 0 and cols > 1

    def body(tokens, norm_gain, gate_weight, up_weight, down_weight):
        part, depth = tokens.shape
        wide = gate_weight.shape[1]
        width = 256 if wide % 512 == 0 else 128
        chunks = wide // (2 * width)
        assert part == 128 and wide % (2 * width) == 0
        lag = hops * (LAG_SUM + LAG_HID)
        slots, places = lag + 2, lag + 2 + KEEP
        banks = -(-LAG_HID * hops // chunks) + 1
        half, full = jnp.bfloat16, jnp.float32
        dma = pltpu.SemaphoreType.DMA
        anywhere = pl.BlockSpec(memory_space=pl.ANY)
        vmem = pl.BlockSpec(memory_space=pltpu.VMEM)
        call = pl.pallas_call(
            functools.partial(kernel, (rows, cols, part, depth, width, chunks)),
            out_shape=jax.ShapeDtypeStruct((part, depth), half),
            in_specs=[anywhere, vmem, anywhere, anywhere, anywhere],
            out_specs=vmem,
            scratch_shapes=[
                pltpu.VMEM((rows, part, depth), half),
                pltpu.VMEM((2 * chunks, depth, 2 * width), half),
                pltpu.VMEM((2 * chunks, width, depth), half),
                pltpu.VMEM((2, slots, part, 2 * width), half),
                pltpu.VMEM((2, STAGES, part, 2 * width), half),
                pltpu.VMEM((part, 2 * width), full),
                pltpu.VMEM((2, places, part, width), half),
                pltpu.VMEM((banks, part, depth), full),
                pltpu.VMEM((part, depth), full),
                pltpu.VMEM((rows, part, depth), half),
                pltpu.VMEM((part, depth), half),
                pltpu.VMEM((8, part), full),
                pltpu.VMEM((cols, 8, part), full),
                pltpu.VMEM((8, part), full),
                pltpu.VMEM((rows, 8, part), full),
                pltpu.VMEM((rows, part, 128), full),
                dma,
                dma((2 * chunks,)), dma((2 * chunks,)), dma((2 * chunks,)),
                dma((rows,)), dma((rows,)), dma, dma((rows,)),
                dma((cols,)), dma((cols,)), dma((rows,)), dma((rows,)),
                dma((2, STAGES)), dma((2, slots)), dma((2, places)), dma((2, places)),
            ],
            compiler_params=pltpu.CompilerParams(
                collective_id=0, has_side_effects=True, vmem_limit_bytes=67_043_328),
        )
        return call(tokens, norm_gain.reshape(1, -1), gate_weight, up_weight, down_weight)

    return body


def solution(mesh):
    placed = (P("row", "col"), P("col"), P("col", "row"), P("col", "row"), P("row", "col"))
    return jax.shard_map(
        make_body(mesh.shape["row"], mesh.shape["col"]),
        mesh=mesh, in_specs=placed, out_specs=P("row", "col"), check_vma=False,
    )
```

profile of v0, /device:TPU:0, one launch (start us, length us, event | category | flops | bytes accessed | tf_op | source)
XLA Modules:
  0.0 300.7 jit_solution(1055066110624119294)
XLA Ops:
  0.0 298.8 %shard_map.55 = bf16[128,2048]{1,0:T(8,128)(2,1)} custom-call(bf16[128,2048]{1,0:T(8,128)(2,1)} %tok.1, f32[1,2048]{1,0:T(1,128)} %bitcast.1, bf16[2048,3584]{1,0:T(8,128)(2,1)} %gate_w.1, bf16[2048,3584]{1,0:T(8,128)(2,1)} %up_w.1, bf16[3584,2048]{1,0:T(8,128)(2,1)} %down_w.1), custom_call_target="tpu_custom_call" | custom-call | tf_op jit(solution)/shard_map/pallas_call | solution.py:347
  298.8 1.9 copy.7
where the time goes:
time: 301 us
  Pallas kernels  299 us (99%)
    pallas_call x1, Pallas kernels, body(): call(tokens, norm_gain.reshape(1, -1), gate_weight, up_weight, down_weight)  299 us

commit v1 on v0

--- a/solution.py
+++ b/solution.py
@@ -9,10 +9,11 @@
 
 MESH = pl.DeviceIdType.MESH
 LAG_SUM = 2
-LAG_HID = 1
+LAG_HID = 2
 STAGES = 4
 KEEP = 2
 PIECES = 4
+AHEAD = 2
 
 
 def exclusive_or(a, b, bits):
@@ -46,10 +47,16 @@
     near = jnp.minimum(spot[0], spot[1])
     far = hops - near
 
+    between = sorted(range(2, rows), key=lambda k: ((k >> 1).bit_count(), k & 1, k))
+    order = [0] + between + [1][: rows - 1]
+
     def mask(i):
         if isinstance(i, int):
-            return 0 if i == 0 else (1 if i == rows - 1 else i + 1)
-        return jnp.where(i == 0, 0, jnp.where(i == rows - 1, 1, i + 1))
+            return order[i]
+        total = 0
+        for at, value in enumerate(order):
+            total = total + jnp.where(i == at, value, 0)
+        return total
 
     def partner(i):
         return exclusive_or(r, mask(i), bits)
@@ -84,7 +91,7 @@
             src_ref=tok, dst_ref=xall.at[i], send_sem=ag_send.at[i], recv_sem=ag_recv.at[i],
             device_id=(partner(i), p), device_id_type=MESH)
 
-    for i in range(1, rows):
+    for i in range(1, min(AHEAD, rows - 1) + 1):
         spread(i).start()
     for j in range(1, chunks):
         for s in (0, 1):
@@ -233,6 +240,11 @@
 
     def step(t, carry):
         first = t - LAG_SUM * near
+        later = first // chunks + AHEAD
+
+        @pl.when((first >= chunks) & (first % chunks == 0) & (later < rows))
+        def _():
+            spread(later).start()
 
         @pl.when((first >= chunks) & (first < units) & (first % chunks == 0))
         def _():

time: 301 us -> 266 us (0.88)
  Pallas kernels: 299 us -> 264 us
    pallas_call x1, Pallas kernels: 299 us -> 264 us  [body(): call(tokens, norm_gain.reshape(1, -1), gate_weight, up_weight, down_weight)]
where the time goes in v1:
time: 266 us
  Pallas kernels  264 us (99%)
    pallas_call x1, Pallas kernels, body(): call(tokens, norm_gain.reshape(1, -1), gate_weight, up_weight, down_weight)  264 us

profile of v1, /device:TPU:0, one launch (start us, length us, event | category | flops | bytes accessed | tf_op | source)
XLA Modules:
  0.0 266.0 jit_solution(12941567601350976025)
XLA Ops:
  0.0 264.1 %shard_map.55 = bf16[128,2048]{1,0:T(8,128)(2,1)} custom-call(bf16[128,2048]{1,0:T(8,128)(2,1)} %tok.1, f32[1,2048]{1,0:T(1,128)} %bitcast.1, bf16[2048,3584]{1,0:T(8,128)(2,1)} %gate_w.1, bf16[2048,3584]{1,0:T(8,128)(2,1)} %up_w.1, bf16[3584,2048]{1,0:T(8,128)(2,1)} %down_w.1), custom_call_target="tpu_custom_call" | custom-call | tf_op jit(solution)/shard_map/pallas_call | solution.py:359
  264.1 1.9 copy.7

commit v2 on v1

v2 whole, which is shorter than its diff:
```python
import functools

import jax
import jax.numpy as jnp
from jax import lax
from jax.experimental import pallas as pl
from jax.experimental.pallas import tpu as pltpu
from jax.sharding import PartitionSpec as P

MESH = pl.DeviceIdType.MESH
LAG_SUM = (2, 2, 2)
LAG_HID = (2, 2, 2)
SPLIT = 1
SPLIT_HID = 1
SPLIT_OUT = 4
STAGES = 4
KEEP = 2
PIECES = 4
FETCH = 2
AHEAD = 2


def exclusive_or(a, b, bits):
    total = a + b
    for bit in range(bits):
        size = 1 << bit
        total = total - 2 * size * (((a // size) % 2) * ((b // size) % 2))
    return total


def lags(hops):
    there = sum(LAG_SUM[h % len(LAG_SUM)] for h in range(hops))
    return there, there + sum(LAG_HID[h % len(LAG_HID)] for h in range(hops))


def kernel(
    plan, tok, gain, gate_w, up_w, down_w, out,
    xall, wgu, wd, gu_in, gu_out, ybuf, hid, acc, own, rs_in, rs_out,
    sq_out, sq_in, tot_out, tot_in, scale,
    own_sem, wg_sem, wu_sem, wd_sem, ag_send, ag_recv, rs_send, rs_recv,
    sq_send, sq_recv, tot_send, tot_recv, gs_send, gs_recv, hs_send, hs_recv,
):
    rows, cols, part, depth, width, chunks = plan
    hops = cols - 1
    units = rows * chunks
    half = chunks * width
    there, lag = lags(hops)
    slots = gu_in.shape[1]
    places = hid.shape[1]
    banks = acc.shape[0]
    bits = rows.bit_length() - 1
    r, p = lax.axis_index("row"), lax.axis_index("col")
    spot = (p, hops - p)
    after = (p + 1, p - 1)
    before = (p - 1, p + 1)
    near = jnp.minimum(spot[0], spot[1])
    far = hops - near

    def sum_lag(q):
        return sum(jnp.where(q > h, LAG_SUM[h % len(LAG_SUM)], 0) for h in range(hops))

    def hidden_lag(q):
        return there + sum(jnp.where(hops - q > h, LAG_HID[h % len(LAG_HID)], 0) for h in range(hops))

    def cut(k, pieces):
        return pl.ds(k * (part // pieces), part // pieces)

    between = sorted(range(2, rows), key=lambda k: ((k >> 1).bit_count(), k & 1, k))
    order = [0] + between + [1][: rows - 1]

    def mask(i):
        if isinstance(i, int):
            return order[i]
        total = 0
        for at, value in enumerate(order):
            total = total + jnp.where(i == at, value, 0)
        return total

    def partner(i):
        return exclusive_or(r, mask(i), bits)

    def weight_copies(s, j):
        at = pl.multiple_of(s * half + j * width, 128)
        c = s * chunks + j
        return (
            pltpu.make_async_copy(gate_w.at[:, pl.ds(at, width)], wgu.at[c, :, pl.ds(0, width)], wg_sem.at[c]),
            pltpu.make_async_copy(up_w.at[:, pl.ds(at, width)], wgu.at[c, :, pl.ds(width, width)], wu_sem.at[c]),
        )

    def down_copy(s, j):
        c = s * chunks + j
        return pltpu.make_async_copy(down_w.at[pl.ds(pl.multiple_of(s * half + j * width, 128), width)], wd.at[c], wd_sem.at[c])

    own_copy = pltpu.make_async_copy(tok, xall.at[0], own_sem)
    own_copy.start()
    for s in (0, 1):
        for one in weight_copies(s, 0):
            one.start()

    barrier = pltpu.get_barrier_semaphore()
    for i in range(1, rows):
        pl.semaphore_signal(barrier, inc=1, device_id=(partner(i), p), device_id_type=MESH)
    for d in range(1, cols):
        pl.semaphore_signal(barrier, inc=1, device_id=(r, (p + d) % cols), device_id_type=MESH)
    pl.semaphore_wait(barrier, rows + cols - 2)

    def spread(i):
        return pltpu.make_async_remote_copy(
            src_ref=tok, dst_ref=xall.at[i], send_sem=ag_send.at[i], recv_sem=ag_recv.at[i],
            device_id=(partner(i), p), device_id_type=MESH)

    for i in range(1, min(AHEAD, rows - 1) + 1):
        spread(i).start()
    for j in range(FETCH):
        for s in (0, 1):
            if j > 0:
                for one in weight_copies(s, j):
                    one.start()
            down_copy(s, j).start()

    def square_copy(d):
        return pltpu.make_async_remote_copy(
            src_ref=sq_out, dst_ref=sq_in.at[d], send_sem=sq_send.at[d], recv_sem=sq_recv.at[d],
            device_id=(r, (p + d) % cols), device_id_type=MESH)

    def total_copy(i):
        return pltpu.make_async_remote_copy(
            src_ref=tot_out, dst_ref=tot_in.at[i], send_sem=tot_send.at[i], recv_sem=tot_recv.at[i],
            device_id=(partner(i), p), device_id_type=MESH)

    own_copy.wait()
    for c in range(depth // 128):
        at = pl.ds(c * 128, 128)
        value = xall[0, :, at].astype(jnp.float32)
        ybuf[0, :, 0:128] = value * value if c == 0 else ybuf[0, :, 0:128] + value * value
        xall[0, :, at] = (value * gain[:, at]).astype(jnp.bfloat16)
    sq_out[...] = jnp.broadcast_to(jnp.sum(ybuf[0, :, 0:128].T, axis=0, keepdims=True), (8, part))
    for d in range(1, cols):
        square_copy(d).start()

    def put_scale(i, total):
        tall = jnp.broadcast_to(total[0:1, :], (128, part)).T
        scale[i] = lax.rsqrt(tall / (depth * cols) + 1e-05)

    def total_squares():
        total = sq_out[...]
        for d in range(1, cols):
            square_copy(d).wait_recv()
            total = total + sq_in[d]
        tot_out[...] = total
        put_scale(0, total)
        for i in range(1, rows):
            total_copy(i).start()

    def sum_copy(s, n, k):
        stage, slot = lax.rem(n, STAGES), lax.rem(n, slots)
        at = cut(k, SPLIT)
        return pltpu.make_async_remote_copy(
            src_ref=gu_out.at[s, stage, at], dst_ref=gu_in.at[s, slot, at],
            send_sem=gs_send.at[s, stage, k], recv_sem=gs_recv.at[s, slot, k],
            device_id=(r, after[s]), device_id_type=MESH)

    def hidden_copy(s, m, k):
        place = lax.rem(m, places)
        at = cut(k, SPLIT_HID)
        return pltpu.make_async_remote_copy(
            src_ref=hid.at[s, place, at], dst_ref=hid.at[s, place, at],
            send_sem=hs_send.at[s, place, k], recv_sem=hs_recv.at[s, place, k],
            device_id=(r, before[s]), device_id_type=MESH)

    def result_copy(i, k):
        at = cut(k, SPLIT_OUT)
        return pltpu.make_async_remote_copy(
            src_ref=rs_out.at[at], dst_ref=rs_in.at[i - 1, at],
            send_sem=rs_send.at[k], recv_sem=rs_recv.at[i - 1, k],
            device_id=(partner(i), p), device_id_type=MESH)

    def multiply(s, t):
        n = t - sum_lag(spot[s])

        @pl.when((n >= 0) & (n < units))
        def _():
            i = n // chunks
            j = n - i * chunks

            @pl.when(i == 0)
            def _():
                for one in weight_copies(s, j):
                    one.wait()

                @pl.when(j < chunks - FETCH)
                def _():
                    for one in weight_copies(s, j + FETCH):
                        one.start()
                    down_copy(s, j + FETCH).start()

            ybuf[s] = jnp.dot(xall[i], wgu[s * chunks + j], preferred_element_type=jnp.float32)

    def sums(s, t):
        q = spot[s]
        n = t - sum_lag(q)
        valid = (n >= 0) & (n < units)

        @pl.when((q < hops) & (n >= STAGES) & (n < units + STAGES))
        def _():
            for k in range(SPLIT):
                sum_copy(s, n - STAGES, k).wait_send()

        @pl.when(valid & (q == 0))
        def _():
            for k in range(SPLIT):
                at = cut(k, SPLIT)
                gu_out[s, lax.rem(n, STAGES), at] = ybuf[s, at].astype(jnp.bfloat16)
                sum_copy(s, n, k).start()

        @pl.when(valid & (q > 0) & (q < hops))
        def _():
            for k in range(SPLIT):
                at = cut(k, SPLIT)
                sum_copy(s, n, k).wait_recv()
                total = ybuf[s, at] + gu_in[s, lax.rem(n, slots), at].astype(jnp.float32)
                gu_out[s, lax.rem(n, STAGES), at] = total.astype(jnp.bfloat16)
                sum_copy(s, n, k).start()

        @pl.when(valid & (q == hops))
        def _():
            i = n // chunks
            every = SPLIT // SPLIT_HID
            for k in range(SPLIT):
                at = cut(k, SPLIT)
                sum_copy(s, n, k).wait_recv()
                factor = scale[i, at]
                for c in range(width // 128):
                    left, right = pl.ds(c * 128, 128), pl.ds(width + c * 128, 128)
                    g = (ybuf[s, at, left] + gu_in[s, lax.rem(n, slots), at, left].astype(jnp.float32)) * factor
                    u = (ybuf[s, at, right] + gu_in[s, lax.rem(n, slots), at, right].astype(jnp.float32)) * factor
                    hid[s, lax.rem(n, places), at, left] = (jax.nn.silu(g) * u).astype(jnp.bfloat16)
                if k % every == every - 1:
                    hidden_copy(s, n, k // every).start()

    def hiddens(s, t):
        q = spot[s]
        m = t - hidden_lag(q)
        valid = (m >= 0) & (m < units)

        @pl.when(valid & (q == 0))
        def _():
            for k in range(SPLIT_HID):
                hidden_copy(s, m, k).wait_recv()

        @pl.when(valid & (q < hops) & (q > 0))
        def _():
            for k in range(SPLIT_HID):
                hidden_copy(s, m, k).wait_recv()
                hidden_copy(s, m, k).start()

    def project(s, t):
        q = spot[s]
        m = t - hidden_lag(q)
        valid = (m >= 0) & (m < units)
        place = lax.rem(jnp.maximum(m, 0), places)

        @pl.when(valid)
        def _():
            i = m // chunks
            j = m - i * chunks
            bank = lax.rem(i, banks)

            @pl.when(i == 0)
            def _():
                down_copy(s, j).wait()

            leads = (q == far) if s == 0 else ((q == far) & (spot[0] != far))
            fresh = leads & (j == 0)
            wide = depth // PIECES
            for c in range(PIECES):
                at = pl.ds(c * wide, wide)
                value = jnp.dot(hid[s, place], wd[s * chunks + j, :, at], preferred_element_type=jnp.float32)

                @pl.when(fresh)
                def _():
                    acc[bank, :, at] = value

                @pl.when(jnp.logical_not(fresh))
                def _():
                    acc[bank, :, at] += value

        @pl.when((q > 0) & (m >= KEEP) & (m < units + KEEP))
        def _():
            for k in range(SPLIT_HID):
                hidden_copy(s, m - KEEP, k).wait_send()

    def prepare(t):
        first = t - sum_lag(near)
        later = first // chunks + AHEAD

        @pl.when((first >= chunks) & (first % chunks == 0) & (later < rows))
        def _():
            spread(later).start()

        @pl.when((first >= chunks) & (first < units) & (first % chunks == 0))
        def _():
            i = first // chunks
            spread(i).wait_recv()
            total_copy(i).wait_recv()
            for c in range(depth // 128):
                at = pl.ds(c * 128, 128)
                xall[i, :, at] = (xall[i, :, at].astype(jnp.float32) * gain[:, at]).astype(jnp.bfloat16)
            put_scale(i, tot_in[i])

    def step(t, carry):
        sums(0, t)
        sums(1, t)
        hiddens(0, t)
        hiddens(1, t)

        @pl.when(t - sum_lag(near) == 1)
        def _():
            total_squares()

        prepare(t + 1)
        multiply(0, t + 1)
        multiply(1, t + 1)
        project(0, t)
        project(1, t)

        last = t - hidden_lag(near)

        @pl.when((last >= 0) & (last < units) & (last % chunks == chunks - 1))
        def _():
            i = last // chunks
            bank = lax.rem(i, banks)

            @pl.when(i == 0)
            def _():
                own[...] = acc[bank]

            @pl.when(i >= 2)
            def _():
                for k in range(SPLIT_OUT):
                    result_copy(i - 1, k).wait_send()

            @pl.when(i > 0)
            def _():
                for k in range(SPLIT_OUT):
                    at = cut(k, SPLIT_OUT)
                    rs_out[at] = acc[bank, at].astype(jnp.bfloat16)
                    result_copy(i, k).start()

            @pl.when(i >= 2)
            def _():
                for k in range(SPLIT_OUT):
                    at = cut(k, SPLIT_OUT)
                    result_copy(i - 1, k).wait_recv()
                    own[at] += rs_in[i - 2, at].astype(jnp.float32)

        return carry

    multiply(0, 0)
    multiply(1, 0)
    lax.fori_loop(0, units + lag + KEEP, step, 0)

    for k in range(SPLIT_OUT):
        at = cut(k, SPLIT_OUT)
        result_copy(rows - 1, k).wait_recv()
        out[at] = (own[at] + rs_in[rows - 2, at].astype(jnp.float32)).astype(jnp.bfloat16)
    for k in range(SPLIT_OUT):
        result_copy(rows - 1, k).wait_send()
    for i in range(1, rows):
        spread(i).wait_send()
        total_copy(i).wait_send()
    for d in range(1, cols):
        square_copy(d).wait_send()


def make_body(rows, cols):
    hops = cols - 1
    assert rows & (rows - 1) == 0 and min(rows, cols) > 1

    def body(tokens, norm_gain, gate_weight, up_weight, down_weight):
        part, depth = tokens.shape
        wide = gate_weight.shape[1]
        width = 256 if wide % 512 == 0 else 128
        chunks = wide // (2 * width)
        assert part == 128 and wide % (2 * width) == 0 and chunks >= FETCH
        there, lag = lags(hops)
        slots, places = lag + 2, lag + 2 + KEEP
        banks = -(-(lag - there) // chunks) + 1
        half, full = jnp.bfloat16, jnp.float32
        dma = pltpu.SemaphoreType.DMA
        anywhere = pl.BlockSpec(memory_space=pl.ANY)
        vmem = pl.BlockSpec(memory_space=pltpu.VMEM)
        call = pl.pallas_call(
            functools.partial(kernel, (rows, cols, part, depth, width, chunks)),
            out_shape=pltpu.VMEM((part, depth), half),
            in_specs=[anywhere, vmem, anywhere, anywhere, anywhere],
            out_specs=vmem,
            scratch_shapes=[
                pltpu.VMEM((rows, part, depth), half),
                pltpu.VMEM((2 * chunks, depth, 2 * width), half),
                pltpu.VMEM((2 * chunks, width, depth), half),
                pltpu.VMEM((2, slots, part, 2 * width), half),
                pltpu.VMEM((2, STAGES, part, 2 * width), half),
                pltpu.VMEM((2, part, 2 * width), full),
                pltpu.VMEM((2, places, part, width), half),
                pltpu.VMEM((banks, part, depth), full),
                pltpu.VMEM((part, depth), full),
                pltpu.VMEM((rows - 1, part, depth), half),
                pltpu.VMEM((part, depth), half),
                pltpu.VMEM((8, part), full),
                pltpu.VMEM((cols, 8, part), full),
                pltpu.VMEM((8, part), full),
                pltpu.VMEM((rows, 8, part), full),
                pltpu.VMEM((rows, part, 128), full),
                dma,
                dma((2 * chunks,)), dma((2 * chunks,)), dma((2 * chunks,)),
                dma((rows,)), dma((rows,)), dma((SPLIT_OUT,)), dma((rows - 1, SPLIT_OUT)),
                dma((cols,)), dma((cols,)), dma((rows,)), dma((rows,)),
                dma((2, STAGES, SPLIT)), dma((2, slots, SPLIT)), dma((2, places, SPLIT_HID)), dma((2, places, SPLIT_HID)),
            ],
            compiler_params=pltpu.CompilerParams(
                collective_id=0, has_side_effects=True, vmem_limit_bytes=66_000_000),
        )
        return call(tokens, norm_gain.reshape(1, -1), gate_weight, up_weight, down_weight)

    return body


def solution(mesh):
    placed = (P("row", "col"), P("col"), P("col", "row"), P("col", "row"), P("row", "col"))
    return jax.shard_map(
        make_body(mesh.shape["row"], mesh.shape["col"]),
        mesh=mesh, in_specs=placed, out_specs=P("row", "col"), check_vma=False,
    )
```

time: 266 us -> 264 us (level)
  no operation moved by 1% of the time
where the time goes in v2:
time: 264 us
  Pallas kernels  263 us (100%)
    pallas_call x1, Pallas kernels, body(): call(tokens, norm_gain.reshape(1, -1), gate_weight, up_weight, down_weight)  263 us

profile of v2, /device:TPU:0, one launch (start us, length us, event | category | flops | bytes accessed | tf_op | source)
XLA Modules:
  0.0 264.2 jit_solution(4380714156642436148)
XLA Ops:
  0.0 263.4 %shard_map.55 = bf16[128,2048]{1,0:T(8,128)(2,1)S(1)} custom-call(bf16[128,2048]{1,0:T(8,128)(2,1)} %tok.1, f32[1,2048]{1,0:T(1,128)} %bitcast.1, bf16[2048,3584]{1,0:T(8,128)(2,1)} %gate_w.1, bf16[2048,3584]{1,0:T(8,128)(2,1)} %up_w.1, bf16[3584,2048]{1,0:T(8,128)(2,1)} %down_w.1), custom_call_target="tpu_custom_call" | custom-call | tf_op jit(solution)/shard_map/pallas_call | solution.py:424
  263.4 0.8 copy.7
